TPU v7x, 32 devices: a whole 2x2x4 slice. The times are simulated.
32 devices in a mesh: tm: 8 (over z, x), rows: 4 (over y, core).
Axes of the slice: x: 2, y: 2, z: 4, core: 2. Of those that a mesh axis runs over, the one named last changes fastest.
Arguments:
- initial_warmth: float32 [1024, 1024], P('rows'), may hold values from -6 to 6
- pattern_choice: int32 [16, 8, 8], P('tm'), may hold values from 0 to 7
- dissipation_tables: float32 [8, 128, 128], replicated, may hold values from -6 to 6
- material_label: int32 [8, 8], replicated, may hold values from 0 to 3
- intercept_kappa: float32 [4], replicated, may hold values from 4 to 8
- sensitivity_coef: float32 [4], replicated, may hold values from -0.5 to 0.5
Outputs:
- warmth_trajectory: float32 [16, 1024, 1024], P('tm', 'rows')
All inputs are finite; a program needn't handle non-finite values.
Results may differ from a plain program's by a relative error of at most 0.0003.
Values sent between devices are 32-bit elements; how exact they have to be, the bound alone decides.
A program may use at most 128 MiB of HBM per device.

v0:
```python
import math
import jax
import jax.numpy as jnp
from jax import lax
from jax.sharding import PartitionSpec as P

TILE = 128
ITERS = 2
TIMESTEP_SIZE = 2.0
ALPHA = 0.05
CROSS_WEIGHT = 1.0 / 64.0
HIGHEST = lax.Precision.HIGHEST


def extended(block, sides, width):
    for axis, dim in sides:
        count = lax.axis_size(axis)
        forward = [(i, i + 1) for i in range(count - 1)]
        backward = [(target, source) for source, target in forward]
        low = lax.ppermute(
            lax.slice_in_dim(block, block.shape[dim] - width, None, axis=dim), axis, forward
        )
        high = lax.ppermute(lax.slice_in_dim(block, 0, width, axis=dim), axis, backward)
        block = jnp.concatenate([low, block, high], axis=dim)
    return block


def shifted(block, axis, distance):
    devices = range(lax.axis_size(axis))
    route = [(i - distance, i) for i in devices if i - distance in devices]
    return lax.ppermute(block, axis, route)


def cosine_tables(length):
    modes = jnp.arange(length, dtype=jnp.int32)[:, None]
    cells = jnp.arange(length, dtype=jnp.int32)[None, :]
    phase = modes * (2 * cells + 1) % (4 * length)
    forward = jnp.cos(phase.astype(jnp.float32) * (math.pi / (2 * length)))
    weights = jnp.where(jnp.arange(length) == 0, 1.0, 2.0).astype(jnp.float32) / length
    inverse = forward.T * weights[None, :]
    return (forward, inverse)


def along_last(values, table):
    array_extent = values.shape
    flat = jnp.dot(
        values.reshape(-1, array_extent[-1]),
        table.T,
        precision=HIGHEST,
        preferred_element_type=jnp.float32,
    )
    return flat.reshape(array_extent[:-1] + (table.shape[0],))


def along_rows(values, table):
    return jnp.einsum("kn,afnc->afkc", table, values, precision=HIGHEST)


def fourier_forward(values):
    count = values.shape[0]
    index = jnp.arange(count, dtype=jnp.int32)
    phase = (index[:, None] * index[None, :] % count).astype(jnp.float32) * (2.0 * math.pi / count)
    table = jnp.concatenate([jnp.cos(phase), -jnp.sin(phase)], 0)
    flat = jnp.dot(
        table, values.reshape(count, -1), precision=HIGHEST, preferred_element_type=jnp.float32
    )
    return flat.reshape((2, count) + values.shape[1:])


def fourier_inverse(values):
    count = values.shape[1]
    index = jnp.arange(count, dtype=jnp.int32)
    phase = (index[:, None] * index[None, :] % count).astype(jnp.float32) * (2.0 * math.pi / count)
    table = jnp.concatenate([jnp.cos(phase), -jnp.sin(phase)], 1) / count
    flat = jnp.dot(
        table, values.reshape(2 * count, -1), precision=HIGHEST, preferred_element_type=jnp.float32
    )
    return flat.reshape((count,) + values.shape[2:])


def shifted_solve(spectra, freq_ids, column_ids, total_steps, grid_height, tile_pitch, conduct):
    shrink = ALPHA ** (1.0 / total_steps)
    theta = (freq_ids % total_steps).astype(jnp.float32) * (2.0 * math.pi / total_steps)
    mu_rows = 2.0 - 2.0 * jnp.cos(
        jnp.arange(grid_height).astype(jnp.float32) * (math.pi / grid_height)
    )
    mu_cols = 2.0 - 2.0 * jnp.cos(column_ids.astype(jnp.float32) * (math.pi / tile_pitch))
    real_den = (1.0 - shrink * jnp.cos(theta))[:, None, None] / TIMESTEP_SIZE + conduct * (
        mu_rows[None, :, None] + CROSS_WEIGHT * mu_cols[None, None, :]
    )
    imag_den = (shrink * jnp.sin(theta) / TIMESTEP_SIZE)[:, None, None]
    norm_den = real_den * real_den + imag_den * imag_den
    real_part = spectra[0]
    imag_part = spectra[1]
    solved_re = (real_part * real_den + imag_part * imag_den) / norm_den
    solved_im = (imag_part * real_den - real_part * imag_den) / norm_den
    return jnp.stack([solved_re, solved_im], 0)


def compute_residual(
    warmth_trajectory, initial_warmth, forcing_term, reference_grid, slope_grid, inner_boundaries
):
    extended_grid = extended(warmth_trajectory, (("rows", 1),), 1)
    kappa_local = reference_grid[None] * (1.0 + slope_grid[None] * jnp.tanh(extended_grid))
    upward_current = (
        0.5
        * (kappa_local[:, 1:] + kappa_local[:, :-1])
        * (extended_grid[:, 1:] - extended_grid[:, :-1])
    )
    upward_current = jnp.where(inner_boundaries[None, :, None], upward_current, 0.0)
    centre = extended_grid[:, 1:-1]
    kappa_mid = kappa_local[:, 1:-1]
    lateral_current = CROSS_WEIGHT * (
        0.5 * (kappa_mid[:, :, 1:] + kappa_mid[:, :, :-1]) * (centre[:, :, 1:] - centre[:, :, :-1])
    )
    zero_column = jnp.zeros_like(centre[:, :, :1])
    across = jnp.concatenate([lateral_current, zero_column], 2) - jnp.concatenate(
        [zero_column, lateral_current], 2
    )
    energy_ledger = upward_current[:, 1:] - upward_current[:, :-1] + across
    evolving_warmth = shifted(warmth_trajectory[-1], "tm", 1)
    evolving_warmth = jnp.where(lax.axis_index("tm") == 0, initial_warmth, evolving_warmth)
    former_warmth = jnp.concatenate([evolving_warmth[None], warmth_trajectory[:-1]], 0)
    return forcing_term - (warmth_trajectory - former_warmth) / TIMESTEP_SIZE + energy_ledger


def shards(
    initial_warmth,
    pattern_choice,
    dissipation_tables,
    material_label,
    intercept_kappa,
    sensitivity_coef,
):
    shard_moments = pattern_choice.shape[0]
    slab_tallies, tile_pitch = initial_warmth.shape
    tm_count = lax.axis_size("tm")
    rows_count = lax.axis_size("rows")
    total_steps = shard_moments * tm_count
    grid_height = slab_tallies * rows_count
    tiles_across = tile_pitch // TILE
    first_row = lax.axis_index("rows") * slab_tallies
    local_rows = first_row + jnp.arange(slab_tallies, dtype=jnp.int32)
    chosen = jnp.take(pattern_choice, local_rows // TILE, axis=1)
    pattern_rows = jnp.take(dissipation_tables, local_rows % TILE, axis=1)
    forcing_term = jnp.zeros((shard_moments, slab_tallies, tiles_across, TILE), jnp.float32)
    for pattern in range(dissipation_tables.shape[0]):
        forcing_term = forcing_term + jnp.where(
            (chosen == pattern)[..., None], pattern_rows[pattern][None, :, None, :], 0.0
        )
    forcing_term = forcing_term.reshape(shard_moments, slab_tallies, tile_pitch)
    padded_rows = first_row - 1 + jnp.arange(slab_tallies + 2, dtype=jnp.int32)
    labels = jnp.take(material_label, jnp.clip(padded_rows, 0, grid_height - 1) // TILE, axis=0)
    base_tiles = jnp.zeros(labels.shape, jnp.float32)
    slope_tiles = jnp.zeros(labels.shape, jnp.float32)
    for label in range(intercept_kappa.shape[0]):
        base_tiles = jnp.where(labels == label, intercept_kappa[label], base_tiles)
        slope_tiles = jnp.where(labels == label, sensitivity_coef[label], slope_tiles)
    reference_grid = jnp.repeat(base_tiles, TILE, axis=1)
    slope_grid = jnp.repeat(slope_tiles, TILE, axis=1)
    upper_rows = padded_rows[:-1]
    inner_boundaries = (upper_rows >= 0) & (upper_rows + 1 <= grid_height - 1)
    conduct = jnp.mean(intercept_kappa)
    step_ids = lax.axis_index("tm") * shard_moments + jnp.arange(shard_moments, dtype=jnp.int32)
    amplification = jnp.exp(step_ids.astype(jnp.float32) * (math.log(ALPHA) / total_steps))
    column_fwd, column_inv = cosine_tables(tile_pitch)
    row_fwd, row_inv = cosine_tables(grid_height)
    narrow = tile_pitch // (tm_count * rows_count)
    arrival = jnp.arange(tile_pitch, dtype=jnp.int32)
    strip_of = arrival // (tm_count * narrow)
    block_of = arrival // narrow % tm_count
    mode_order = block_of * (rows_count * narrow) + strip_of * narrow + arrival % narrow
    column_back = jnp.take(column_inv, mode_order, axis=1)
    warmth_trajectory = jnp.broadcast_to(
        initial_warmth[None], (shard_moments, slab_tallies, tile_pitch)
    )
    for sweep in range(ITERS):
        defect_vector = compute_residual(
            warmth_trajectory,
            initial_warmth,
            forcing_term,
            reference_grid,
            slope_grid,
            inner_boundaries,
        )
        scaled = defect_vector * amplification[:, None, None]
        column_modes = along_last(scaled, column_fwd)
        gathered = lax.all_to_all(
            lax.all_to_all(column_modes, "tm", split_axis=2, concat_axis=0, tiled=True),
            "rows",
            split_axis=2,
            concat_axis=1,
            tiled=True,
        )
        column_width = gathered.shape[2]
        column_ids = (
            lax.axis_index("tm") * (rows_count * column_width)
            + lax.axis_index("rows") * column_width
            + jnp.arange(column_width, dtype=jnp.int32)
        )
        spectra = along_rows(fourier_forward(gathered), row_fwd)
        freq_ids = jnp.arange(total_steps, dtype=jnp.int32)
        solved = shifted_solve(
            spectra, freq_ids, column_ids, total_steps, grid_height, tile_pitch, conduct
        )
        solved = along_rows(solved, row_inv)
        field = fourier_inverse(solved)
        correction_delta = lax.all_to_all(
            lax.all_to_all(field, "tm", split_axis=0, concat_axis=2, tiled=True),
            "rows",
            split_axis=1,
            concat_axis=2,
            tiled=True,
        )
        correction_delta = along_last(correction_delta, column_back)
        warmth_trajectory = warmth_trajectory + correction_delta / amplification[:, None, None]
    return warmth_trajectory


def solution(mesh):
    in_specs = (P("rows", None), P("tm", None, None), P(), P(), P(), P())
    out_specs = P("tm", "rows", None)
    return jax.shard_map(shards, mesh=mesh, in_specs=in_specs, out_specs=out_specs, check_vma=False)
```

profile of v0, /device:TPU:0, one launch (start us, length us, event | category | flops | bytes accessed | tf_op | source)
XLA Modules:
  0.0 817.1 jit_solution(5478636304248418031)
XLA Ops:
  0.0 6.0 collective-permute-start
  12.4 2.9 subtract_multiply_fusion
  15.9 2.4 gather_fusion.1
  31.0 2.1 broadcast_in_dim.320
  41.0 1.9 broadcast_in_dim.344
  43.0 2.2 broadcast_in_dim.345
  45.2 1.9 broadcast_in_dim.350
  47.2 2.2 broadcast_in_dim.351
  49.4 1.9 broadcast_in_dim.356
  51.3 2.2 broadcast_in_dim.357
  55.9 2.6 select_select_fusion.1
  58.6 2.7 select_select_fusion
  61.3 5.9 select_add_fusion
  75.1 26.0 %fusion.29 = f32[2,256,1024]{2,1,0:T(8,128)} fusion(f32[2,257,1024]{2,1,0:T(8,128)S(1)} %fusion.46, f32[2,256,1024]{2,1,0:T(8,128)S(1)} %copy-done.13, f32[1,256,1024]{2,1,0:T(8,128)S(1)} %bitcast.225, f32[1,256,1024]{2,1,0:T(8,128)S(1)} %select_bitcast_fusion.2, s32[1024]{0:T(1024)S(1)} %copy-done.15, f32[2,256,1023]{2,1,0:T(8,128)S(1)} %fusion.91, ...), kind=kOutput, calls=%fused_computation.44 | convolution fusion | flops 6461849600 | bytes 13636096 | tf_op jit(solution)/shard_map/dot_general | solution.py:46
  101.0 2.8 copy.60
  103.9 52.3 %all_to_all.132 = f32[2,256,1024]{1,0,2:T(2,128)S(1)} all-to-all(f32[2,256,1024]{1,0,2:T(2,128)S(1)} %copy.60), channel_id=1, replica_groups=mesh['tm'=8,'rows'=4] {'tm'}, dimensions={2} | all-to-all | bytes 4194304 | tf_op jit(solution)/shard_map/all_to_all | solution.py:189
  156.4 1.8 copy.62
  158.2 3.1 copy.63
  161.3 4.6 all-to-all-start.1
  167.6 23.9 %all-to-all-done.1 = f32[16,256,128]{1,0,2:T(8,128)S(1)} async-done(((f32[16,256,128]{1,0,2:T(8,128)}), f32[16,256,128]{1,0,2:T(8,128)S(1)}, u32[]{:S(2)}, u32[]{:S(2)}) %all-to-all-start.1) | async-done | bytes 2097184 | tf_op jit(solution)/shard_map/all_to_all | solution.py:188
  191.6 4.7 copy.65
  196.2 6.0 reshape.506
  202.2 4.8 dot_general.61
  207.1 5.5 copy.66
  212.5 3.4 fusion.109
  215.9 33.4 %fusion.53 = f32[2,16,1024,32]{2,3,1,0:T(8,128)S(1)} fusion(f32[2,16,1024,32]{2,1,3,0:T(8,128)S(1)} %fusion.109, s32[1024]{0:T(1024)S(1)} %copy-done.15), kind=kOutput, calls=%fused_computation.74 | convolution fusion | flops 12899581952 | bytes 8392704 | tf_op jit(solution)/shard_map/kn,afnc->afkc/dot_general | solution.py:56
  250.5 30.6 %fusion.68 = f32[2,16,1024,32]{2,3,1,0:T(8,128)} fusion(f32[1,16,1024,32]{2,3,1,0:T(8,128)S(1)} %get-tuple-element.13, f32[1,16,1024,32]{2,3,1,0:T(8,128)S(1)} %get-tuple-element.12, f32[1024]{0:T(1024)S(1)} %select_multiply_fusion, s32[1024]{0:T(1024)S(1)} %copy-done.15), kind=kOutput, calls=%fused_computation.77 | convolution fusion | flops 12901679104 | bytes 8396800 | tf_op jit(solution)/shard_map/kn,afnc->afkc/dot_general | solution.py:56
  281.2 10.4 %copy.69 = f32[2,16,1024,32]{3,2,1,0:T(8,128)} copy(f32[2,16,1024,32]{2,3,1,0:T(8,128)} %fusion.68) | data formatting | bytes 8388608 | tf_op jit(solution)/shard_map/kn,afnc->afkc/transpose | solution.py:56
  291.6 11.6 %reshape.507 = f32[32,32768]{1,0:T(8,128)} reshape(f32[2,16,1024,32]{3,2,1,0:T(8,128)} %copy.69) | data formatting | bytes 8388608 | tf_op jit(solution)/shard_map/reshape | solution.py:76
  303.3 9.8 %dot_general.66 = f32[1024,32,32]{1,0,2:T(8,128)} reshape(f32[32768,32]{0,1:T(8,128)} %bitcast.226) | data formatting | bytes 8388608 | tf_op jit(solution)/shard_map/dot_general | solution.py:75
  313.1 11.8 %copy.70 = f32[1024,32,32]{0,2,1:T(8,128)} copy(f32[1024,32,32]{1,0,2:T(8,128)} %dot_general.66) | data formatting | bytes 8388608 | tf_op jit(solution)/shard_map/dot_general | solution.py:75
  324.9 4.1 fusion.165
  330.3 51.1 %all_to_all.133 = f32[16,1024,32]{1,2,0:T(8,128)S(1)} all-to-all(f32[16,1024,32]{1,2,0:T(8,128)S(1)} %copy.71), channel_id=1, replica_groups=mesh['tm'=8,'rows'=4] {'tm'}, dimensions={0} | all-to-all | bytes 4194304 | tf_op jit(solution)/shard_map/all_to_all | solution.py:209
  381.6 2.4 copy.73
  384.0 4.0 all-to-all-start.3
  388.1 16.2 %fusion.8 = f32[1024,1024]{0,1:T(8,128)} fusion(f32[1024]{0:T(1024)S(1)} %select_multiply_fusion, s32[1024]{0:T(1024)S(1)} %copy-done.15), kind=kLoop, calls=%fused_computation.23 | loop fusion | flops 15728640 | bytes 4202496 | tf_op jit(solution)/shard_map/mul | solution.py:40
  404.3 8.5 %gather_fusion.3 = f32[1024,1024]{1,0:T(8,128)} fusion(f32[1024,1024]{0,1:T(8,128)} %fusion.8, s32[1024]{0:T(1024)S(1)} %broadcast_clamp_fusion), kind=kCustom, calls=%fused_computation.3 | custom fusion | bytes 8392704 | tf_op jit(solution)/shard_map/jit(_take)/gather | solution.py:173
  416.2 7.3 divide_add_fusion.1
  423.5 1.7 collective-permute-start.4
  426.7 3.5 collective-permute-start.3
  432.7 19.5 %collective-permute-done.3 = f32[256,1024]{1,0:T(8,128)S(1)} collective-permute-done((f32[256,1024]{1,0:T(8,128)S(1)}, f32[256,1024]{1,0:T(8,128)S(1)}, u32[]{:S(2)}, u32[]{:S(2)}) %collective-permute-start.3) | collective-permute-done | bytes 1048608 | tf_op jit(solution)/shard_map/ppermute | solution.py:31
  452.4 25.7 %fusion.27 = f32[2,256,1024]{2,1,0:T(8,128)} fusion(f32[2,257,1024]{2,1,0:T(8,128)S(1)} %fusion.43, f32[2,256,1024]{2,1,0:T(8,128)S(1)} %copy-done.14, f32[2,256,1024]{2,1,0:T(8,128)S(1)} %divide_add_fusion.1, f32[1,256,1024]{2,1,0:T(8,128)S(1)} %get-tuple-element.15, f32[1,256,1024]{2,1,0:T(8,128)S(1)} %select_bitcast_fusion.1, ...), kind=kOutput, calls=%fused_computation.42 | convolution fusion | flops 6461849600 | bytes 14684672 | tf_op jit(solution)/shard_map/dot_general | solution.py:46
  478.2 4.1 copy.77
  482.3 54.1 %all_to_all.134 = f32[2,256,1024]{1,0,2:T(2,128)S(1)} all-to-all(f32[2,256,1024]{1,0,2:T(2,128)} %copy.77), channel_id=1, replica_groups=mesh['tm'=8,'rows'=4] {'tm'}, dimensions={2} | all-to-all | bytes 4194304 | tf_op jit(solution)/shard_map/all_to_all | solution.py:189
  537.9 2.9 copy.79
  540.8 3.0 copy.80
  543.8 30.4 %all_to_all.135 = f32[16,256,128]{1,0,2:T(8,128)} all-to-all(f32[16,256,128]{1,0,2:T(8,128)} %copy.80), channel_id=1, replica_groups=mesh['tm'=8,'rows'=4] {'rows'}, dimensions={2} | all-to-all | bytes 4194304 | tf_op jit(solution)/shard_map/all_to_all | solution.py:188
  574.2 6.3 copy.82
  580.5 7.0 reshape.508
  587.5 6.0 dot_general.72
  593.5 6.4 copy.83
  599.9 5.0 fusion.107
  604.9 33.5 %fusion.58 = f32[2,16,1024,32]{2,3,1,0:T(8,128)S(1)} fusion(f32[2,16,1024,32]{2,1,3,0:T(8,128)S(1)} %fusion.107, s32[1024]{0:T(1024)S(1)} %copy-done.15), kind=kOutput, calls=%fused_computation.75 | convolution fusion | flops 12899581952 | bytes 8392704 | tf_op jit(solution)/shard_map/kn,afnc->afkc/dot_general | solution.py:56
  639.5 30.6 %fusion.63 = f32[2,16,1024,32]{2,3,1,0:T(8,128)} fusion(f32[1,16,1024,32]{2,3,1,0:T(8,128)S(1)} %get-tuple-element.11, f32[1,16,1024,32]{2,3,1,0:T(8,128)S(1)} %get-tuple-element.10, f32[1024]{0:T(1024)S(1)} %select_multiply_fusion, s32[1024]{0:T(1024)S(1)} %copy-done.15), kind=kOutput, calls=%fused_computation.76 | convolution fusion | flops 12901679104 | bytes 8396800 | tf_op jit(solution)/shard_map/kn,afnc->afkc/dot_general | solution.py:56
  670.2 10.4 %copy.86 = f32[2,16,1024,32]{3,2,1,0:T(8,128)} copy(f32[2,16,1024,32]{2,3,1,0:T(8,128)} %fusion.63) | data formatting | bytes 8388608 | tf_op jit(solution)/shard_map/kn,afnc->afkc/transpose | solution.py:56
  680.6 11.7 %reshape.509 = f32[32,32768]{1,0:T(8,128)} reshape(f32[2,16,1024,32]{3,2,1,0:T(8,128)} %copy.86) | data formatting | bytes 8388608 | tf_op jit(solution)/shard_map/reshape | solution.py:76
  692.4 9.8 %dot_general.77 = f32[1024,32,32]{1,0,2:T(8,128)} reshape(f32[32768,32]{0,1:T(8,128)} %bitcast.227) | data formatting | bytes 8388608 | tf_op jit(solution)/shard_map/dot_general | solution.py:75
  702.2 11.8 %copy.87 = f32[1024,32,32]{0,2,1:T(8,128)} copy(f32[1024,32,32]{1,0,2:T(8,128)} %dot_general.77) | data formatting | bytes 8388608 | tf_op jit(solution)/shard_map/dot_general | solution.py:75
  714.0 4.1 fusion.163
  719.4 51.5 %all_to_all.136 = f32[16,1024,32]{1,2,0:T(8,128)S(1)} all-to-all(f32[16,1024,32]{1,2,0:T(8,128)S(1)} %copy.88), channel_id=1, replica_groups=mesh['tm'=8,'rows'=4] {'tm'}, dimensions={0} | all-to-all | bytes 4194304 | tf_op jit(solution)/shard_map/all_to_all | solution.py:209
  772.3 4.1 copy.90
  776.4 29.5 %all_to_all.137 = f32[2,1024,256]{2,0,1:T(2,128)S(1)} all-to-all(f32[2,1024,256]{2,0,1:T(2,128)} %copy.90), channel_id=1, replica_groups=mesh['tm'=8,'rows'=4] {'rows'}, dimensions={1} | all-to-all | bytes 4194304 | tf_op jit(solution)/shard_map/all_to_all | solution.py:208
  806.3 1.9 copy-done.11
  808.2 8.6 %divide_add_fusion = f32[2,256,1024]{2,1,0:T(8,128)} fusion(f32[2,256,1024]{2,1,0:T(8,128)S(1)} %divide_add_fusion.1, f32[2]{0:T(128)S(1)} %multiply_exponential_fusion, f32[2,256,1024]{2,1,0:T(8,128)S(1)} %bitcast.264, f32[1024,1024]{1,0:T(8,128)S(1)} %copy-done.11, pred[1024]{0:T(1024)(128)(4,1)S(1)} %compare_and_fusion), kind=kOutput, calls=%fused_computation.121 | convolution fusion | flops 6444548096 | bytes 10486792 | tf_op jit(solution)/shard_map/dot_general | solution.py:46
  (137 shorter events, 54.4 us)
Async XLA Ops:
  0.0 15.9 %copy-start = (f32[8,128,128]{2,1,0:T(8,128)S(1)}, f32[8,128,128]{2,1,0:T(8,128)}, u32[]{:S(2)}) copy-start(f32[8,128,128]{2,1,0:T(8,128)} %param.8) | copy-start | bytes 1572868
  0.0 73.5 %collective-permute-start = (f32[256,1024]{1,0:T(8,128)}, f32[256,1024]{1,0:T(8,128)}, u32[]{:S(2)}, u32[]{:S(2)}) collective-permute-start(f32[256,1024]{1,0:T(8,128)} %param.6), channel_id=1, source_target_pairs={{0,4},{4,8},{8,12},{12,16},{16,20},{20,24},{24,28},{1,5},{5,9},{9,... | collective-permute-start | bytes 3145736 | tf_op jit(solution)/shard_map/ppermute | solution.py:31
  7.4 62.2 %collective-permute-start.1 = (f32[2,1,1024]{2,1,0:T(1,128)}, f32[2,1,1024]{2,1,0:T(1,128)S(1)}, u32[]{:S(2)}, u32[]{:S(2)}) collective-permute-start(f32[2,1,1024]{2,1,0:T(1,128)} %broadcast_in_dim.376), channel_id=1, source_target_pairs={{0,1},{1,2},{2,3},{4,5},{5,6},{6,7},{8,9},{9,10},{10,11},{12,13},{... | collective-permute-start | bytes 24584 | tf_op jit(solution)/shard_map/ppermute | solution.py:20
  9.4 60.1 %collective-permute-start.2 = (f32[2,1,1024]{2,1,0:T(1,128)}, f32[2,1,1024]{2,1,0:T(1,128)S(1)}, u32[]{:S(2)}, u32[]{:S(2)}) collective-permute-start(f32[2,1,1024]{2,1,0:T(1,128)} %broadcast_in_dim.377), channel_id=1, source_target_pairs={{1,0},{2,1},{3,2},{5,4},{6,5},{7,6},{9,8},{10,9},{11,10},{13,12},{... | collective-permute-start | bytes 24584 | tf_op jit(solution)/shard_map/ppermute | solution.py:23
  25.5 1.4 copy-start.2
  42.9 10.6 %copy-start.16 = (s32[258]{0:T(512)S(1)}, s32[258]{0:T(512)}, u32[]{:S(2)}) copy-start(s32[258]{0:T(512)} %fusion.170) | copy-start | bytes 3100
  42.9 10.6 %copy-start.19 = (f32[4]{0:T(128)S(1)}, f32[4]{0:T(128)}, u32[]{:S(2)}) copy-start(f32[4]{0:T(128)} %param.10) | copy-start | bytes 52
  42.9 11.2 %copy-start.18 = (f32[4]{0:T(128)S(1)}, f32[4]{0:T(128)}, u32[]{:S(2)}) copy-start(f32[4]{0:T(128)} %param.11) | copy-start | bytes 52
  42.9 11.9 %copy-start.17 = (s32[258]{0:T(512)S(1)}, s32[258]{0:T(512)}, u32[]{:S(2)}) copy-start(s32[258]{0:T(512)} %iota_add_fusion) | copy-start | bytes 3100
  43.0 11.9 %copy-start.3 = (s32[8,8]{1,0:T(8,128)S(1)}, s32[8,8]{1,0:T(8,128)}, u32[]{:S(2)}) copy-start(s32[8,8]{1,0:T(8,128)} %param.9) | copy-start | bytes 772
  45.2 10.7 %copy-start.20 = (pred[258]{0:T(512)(128)(4,1)S(1)}, pred[258]{0:T(512)(128)(4,1)}, u32[]{:S(2)}) copy-start(pred[258]{0:T(512)(128)(4,1)} %compare_and_fusion.1) | copy-start | bytes 778
  67.8 2.0 copy-start.6
  68.2 1.4 copy-start.4
  69.5 1.2 copy-start.8
  70.8 1.2 copy-start.12
  73.5 1.6 copy-start.13
  73.5 1.6 copy-start.15
  161.3 30.2 %all-to-all-start.1 = ((f32[16,256,128]{1,0,2:T(8,128)}), f32[16,256,128]{1,0,2:T(8,128)S(1)}, u32[]{:S(2)}, u32[]{:S(2)}) async-start(f32[16,256,128]{1,0,2:T(8,128)} %copy.63), calls=%async_computation.1 | async-start | bytes 4194304 | tf_op jit(solution)/shard_map/all_to_all | solution.py:188
  384.0 29.6 %all-to-all-start.3 = ((f32[2,1024,256]{2,0,1:T(2,128)}), f32[2,1024,256]{2,0,1:T(2,128)S(1)}, u32[]{:S(2)}, u32[]{:S(2)}) async-start(f32[2,1024,256]{2,0,1:T(2,128)} %copy.73), calls=%async_computation.3 | async-start | bytes 4194304 | tf_op jit(solution)/shard_map/all_to_all | solution.py:208
  413.7 2.2 copy-start.10
  413.8 2.4 copy-start.5
  423.5 6.8 copy-start.7
  423.5 6.8 copy-start.9
  423.5 6.7 collective-permute-start.4
  425.3 5.0 collective-permute-start.5
  426.7 25.5 %collective-permute-start.3 = (f32[256,1024]{1,0:T(8,128)S(1)}, f32[256,1024]{1,0:T(8,128)S(1)}, u32[]{:S(2)}, u32[]{:S(2)}) collective-permute-start(f32[256,1024]{1,0:T(8,128)S(1)} %get-tuple-element.14), channel_id=1, source_target_pairs={{0,4},{4,8},{8,12},{12,16},{16,20},{20,24},{24,28},{1,5},{5,9},{9,... | collective-permute-start | bytes 3145736 | tf_op jit(solution)/shard_map/ppermute | solution.py:31
  432.7 19.7 %copy-start.14 = (f32[2,256,1024]{2,1,0:T(8,128)S(1)}, f32[2,256,1024]{2,1,0:T(8,128)}, u32[]{:S(2)}) copy-start(f32[2,256,1024]{2,1,0:T(8,128)} %select_add_fusion) | copy-start | bytes 6291460
  806.0 2.2 copy-start.11
  808.2 8.6 %copy-start.1 = (f32[8,128,128]{2,1,0:T(8,128)S(1)}, f32[8,128,128]{2,1,0:T(8,128)}, u32[]{:S(2)}) copy-start(f32[8,128,128]{2,1,0:T(8,128)} %param.8) | copy-start | bytes 1572868
where the time goes:
time: 825 us; the launch traced here: 817 us
  blocking collectives  269 us (33%)
  local copies, waits for them, and re-layouts  224 us (27%)
  matrix products  212 us (26%)
  waiting for transfers between devices  44.3 us (5%)
  other arithmetic  42 us (5%)
  starting transfers between devices  23.8 us (3%)
    dot_general x4, matrix products, along_rows(): return jnp.einsum('kn,afnc->afkc', table, values, precision=HIGHEST)  128 us
    all_to_all x2, blocking collectives, shards(): lax.all_to_all(column_modes, 'tm', split_axis=2, concat_axis=0, tiled=True)  106 us
    all_to_all x2, blocking collectives, shards(): lax.all_to_all(field, 'tm', split_axis=0, concat_axis=2, tiled=True)  103 us
    dot_general x4, matrix products, along_last(): jnp.dot(values.reshape(-1, array_extent[-1]), table.T, precision=HIGHEST,...  67.6 us
    dot_general x6, local copies, waits for them, and re-layouts, fourier_inverse(): jnp.dot(table, values.reshape(2 * count, -1), precision=HIGHEST, preferre...  45.7 us
    all_to_all x1, blocking collectives, shards(): lax.all_to_all(lax.all_to_all(column_modes, 'tm', split_axis=2, concat_ax...  30.4 us
    all_to_all x1, blocking collectives, shards(): lax.all_to_all(lax.all_to_all(field, 'tm', split_axis=0, concat_axis=2, t...  29.5 us
    broadcast_in_dim x25, local copies, waits for them, and re-layouts, shards(): jnp.where((chosen == pattern)[..., None], pattern_rows[pattern][None, :,...  25.2 us
  transfers between devices with their start and end apart: 8, of which 3 were waited for; matrix products, arithmetic and copies ran while one was open for 11% of the time, Pallas kernels for 0%

commit v1 on v0

--- a/solution.py
+++ b/solution.py
@@ -185,12 +185,20 @@
         )
         scaled = defect_vector * amplification[:, None, None]
         column_modes = along_last(scaled, column_fwd)
-        gathered = lax.all_to_all(
-            lax.all_to_all(column_modes, "tm", split_axis=2, concat_axis=0, tiled=True),
-            "rows",
-            split_axis=2,
-            concat_axis=1,
-            tiled=True,
+        gathered = jnp.concatenate(
+            lax.all_to_all(
+                jnp.stack(
+                    jnp.split(
+                        lax.all_to_all(column_modes, "tm", split_axis=2, concat_axis=0, tiled=True),
+                        lax.axis_size("rows"),
+                        axis=2,
+                    )
+                ),
+                "rows",
+                0,
+                0,
+            ),
+            axis=1,
         )
         column_width = gathered.shape[2]
         column_ids = (

time: 825 us -> 856 us (1.038)
  local copies, waits for them, and re-layouts: 224 us -> 252 us
    another operation x0 -> x12, local copies, waits for them, and re-layouts: none -> 45.7 us  [the longest x10 32.8 us: shards(): jnp.stack(jnp.split(lax.all_to_all(column_modes, 'tm', split_axis=2, conc...]
    all_to_all x2 -> x0, local copies, waits for them, and re-layouts: 11 us -> none  [shards(): lax.all_to_all(lax.all_to_all(column_modes, 'tm', split_axis=2, concat_ax...]
where the time goes in v1:
time: 856 us; the launch traced here: 848 us
  blocking collectives  268 us (31%)
  local copies, waits for them, and re-layouts  252 us (29%)
  matrix products  213 us (25%)
  other arithmetic  46.1 us (5%)
  waiting for transfers between devices  44.1 us (5%)
  starting transfers between devices  24 us (3%)
    dot_general x4, matrix products, along_rows(): return jnp.einsum('kn,afnc->afkc', table, values, precision=HIGHEST)  128 us
    all_to_all x2, blocking collectives, shards(): lax.all_to_all(column_modes, 'tm', split_axis=2, concat_axis=0, tiled=True)  107 us
    all_to_all x2, blocking collectives, shards(): lax.all_to_all(field, 'tm', split_axis=0, concat_axis=2, tiled=True)  103 us
    dot_general x4, matrix products, along_last(): jnp.dot(values.reshape(-1, array_extent[-1]), table.T, precision=HIGHEST,...  67.8 us
    dot_general x6, local copies, waits for them, and re-layouts, fourier_inverse(): jnp.dot(table, values.reshape(2 * count, -1), precision=HIGHEST, preferre...  45.6 us
    another operation x10, local copies, waits for them, and re-layouts, shards(): jnp.stack(jnp.split(lax.all_to_all(column_modes, 'tm', split_axis=2, conc...  32.8 us
    all_to_all x1, blocking collectives, shards(): lax.all_to_all(lax.all_to_all(field, 'tm', split_axis=0, concat_axis=2, t...  29.5 us
    all_to_all x1, blocking collectives, shards(): lax.all_to_all(jnp.stack(jnp.split(lax.all_to_all(column_modes, 'tm', spl...  29 us
  transfers between devices with their start and end apart: 8, of which 3 were waited for; matrix products, arithmetic and copies ran while one was open for 11% of the time, Pallas kernels for 0%

profile of v1, /device:TPU:0, one launch (start us, length us, event | category | flops | bytes accessed | tf_op | source)
XLA Modules:
  0.0 847.9 jit_solution(5942086468273990027)
XLA Ops:
  0.0 6.0 collective-permute-start
  12.5 2.9 subtract_multiply_fusion
  16.0 2.4 gather_fusion.1
  42.7 2.3 broadcast_in_dim.345
  47.0 2.2 broadcast_in_dim.351
  51.1 2.2 broadcast_in_dim.357
  55.8 2.7 select_select_fusion.1
  58.5 2.5 select_select_fusion
  61.1 5.9 select_add_fusion
  74.8 26.2 %fusion.29 = f32[2,256,1024]{2,1,0:T(8,128)} fusion(f32[2,257,1024]{2,1,0:T(8,128)S(1)} %fusion.46, f32[2,256,1024]{2,1,0:T(8,128)S(1)} %copy-done.14, f32[1,256,1024]{2,1,0:T(8,128)S(1)} %bitcast.239, f32[1,256,1024]{2,1,0:T(8,128)S(1)} %select_bitcast_fusion.2, s32[1024]{0:T(1024)S(1)} %copy-done.16, f32[2,256,1023]{2,1,0:T(8,128)S(1)} %fusion.91, ...), kind=kOutput, calls=%fused_computation.44 | convolution fusion | flops 6461849600 | bytes 13636096 | tf_op jit(solution)/shard_map/dot_general | solution.py:46
  101.0 2.8 copy.62
  103.9 52.3 %all_to_all.112 = f32[2,256,1024]{1,0,2:T(2,128)S(1)} all-to-all(f32[2,256,1024]{1,0,2:T(2,128)S(1)} %copy.62), channel_id=1, replica_groups=mesh['tm'=8,'rows'=4] {'tm'}, dimensions={2} | all-to-all | bytes 4194304 | tf_op jit(solution)/shard_map/all_to_all | solution.py:192
  159.7 5.0 slice_bitcast_fusion.7
  164.7 2.2 copy.65
  166.8 2.3 copy.66
  169.2 3.0 copy.67
  173.5 2.8 pad_maximum_fusion
  176.3 4.6 all-to-all-start.1
  182.4 24.1 %all-to-all-done.1 = f32[4,16,256,32]{2,3,1,0:T(8,128)S(1)} async-done(((f32[4,16,256,32]{2,3,1,0:T(8,128)}), f32[4,16,256,32]{2,3,1,0:T(8,128)S(1)}, u32[]{:S(2)}, u32[]{:S(2)}) %all-to-all-start.1) | async-done | bytes 2097184 | tf_op jit(solution)/shard_map/all_to_all | solution.py:189
  206.5 4.7 copy.69
  211.3 6.0 reshape_reshape.6
  217.3 4.8 dot_general.61
  222.1 5.5 copy.70
  227.6 3.4 fusion.109
  231.0 33.4 %fusion.53 = f32[2,16,1024,32]{2,3,1,0:T(8,128)S(1)} fusion(f32[2,16,1024,32]{2,1,3,0:T(8,128)S(1)} %fusion.109, s32[1024]{0:T(1024)S(1)} %copy-done.16), kind=kOutput, calls=%fused_computation.74 | convolution fusion | flops 12899581952 | bytes 8392704 | tf_op jit(solution)/shard_map/kn,afnc->afkc/dot_general | solution.py:56
  265.6 30.6 %fusion.68 = f32[2,16,1024,32]{2,3,1,0:T(8,128)} fusion(f32[1,16,1024,32]{2,3,1,0:T(8,128)S(1)} %get-tuple-element.13, f32[1,16,1024,32]{2,3,1,0:T(8,128)S(1)} %get-tuple-element.12, f32[1024]{0:T(1024)S(1)} %select_multiply_fusion, s32[1024]{0:T(1024)S(1)} %copy-done.16), kind=kOutput, calls=%fused_computation.77 | convolution fusion | flops 12901679104 | bytes 8396800 | tf_op jit(solution)/shard_map/kn,afnc->afkc/dot_general | solution.py:56
  296.2 10.5 %copy.73 = f32[2,16,1024,32]{3,2,1,0:T(8,128)} copy(f32[2,16,1024,32]{2,3,1,0:T(8,128)} %fusion.68) | data formatting | bytes 8388608 | tf_op jit(solution)/shard_map/kn,afnc->afkc/transpose | solution.py:56
  306.6 11.6 %reshape.505 = f32[32,32768]{1,0:T(8,128)} reshape(f32[2,16,1024,32]{3,2,1,0:T(8,128)} %copy.73) | data formatting | bytes 8388608 | tf_op jit(solution)/shard_map/reshape | solution.py:76
  318.3 9.9 %dot_general.66 = f32[1024,32,32]{1,0,2:T(8,128)} reshape(f32[32768,32]{0,1:T(8,128)} %bitcast.240) | data formatting | bytes 8388608 | tf_op jit(solution)/shard_map/dot_general | solution.py:75
  328.1 11.7 %copy.74 = f32[1024,32,32]{0,2,1:T(8,128)} copy(f32[1024,32,32]{1,0,2:T(8,128)} %dot_general.66) | data formatting | bytes 8388608 | tf_op jit(solution)/shard_map/dot_general | solution.py:75
  339.9 4.1 fusion.165
  345.3 51.1 %all_to_all.113 = f32[16,1024,32]{1,2,0:T(8,128)S(1)} all-to-all(f32[16,1024,32]{1,2,0:T(8,128)S(1)} %copy.75), channel_id=1, replica_groups=mesh['tm'=8,'rows'=4] {'tm'}, dimensions={0} | all-to-all | bytes 4194304 | tf_op jit(solution)/shard_map/all_to_all | solution.py:217
  396.6 2.4 copy.77
  399.0 3.8 all-to-all-start.3
  402.9 16.2 %fusion.8 = f32[1024,1024]{0,1:T(8,128)} fusion(f32[1024]{0:T(1024)S(1)} %select_multiply_fusion, s32[1024]{0:T(1024)S(1)} %copy-done.16), kind=kLoop, calls=%fused_computation.23 | loop fusion | flops 15728640 | bytes 4202496 | tf_op jit(solution)/shard_map/mul | solution.py:40
  419.1 8.6 %gather_fusion.3 = f32[1024,1024]{1,0:T(8,128)} fusion(f32[1024,1024]{0,1:T(8,128)} %fusion.8, s32[1024]{0:T(1024)S(1)} %broadcast_clamp_fusion), kind=kCustom, calls=%fused_computation.3 | custom fusion | bytes 8392704 | tf_op jit(solution)/shard_map/jit(_take)/gather | solution.py:173
  431.0 7.3 divide_add_fusion.1
  441.6 3.8 collective-permute-start.3
  447.9 19.3 %collective-permute-done.3 = f32[256,1024]{1,0:T(8,128)S(1)} collective-permute-done((f32[256,1024]{1,0:T(8,128)S(1)}, f32[256,1024]{1,0:T(8,128)S(1)}, u32[]{:S(2)}, u32[]{:S(2)}) %collective-permute-start.3) | collective-permute-done | bytes 1048608 | tf_op jit(solution)/shard_map/ppermute | solution.py:31
  467.3 25.7 %fusion.27 = f32[2,256,1024]{2,1,0:T(8,128)} fusion(f32[2,257,1024]{2,1,0:T(8,128)S(1)} %fusion.43, f32[2,256,1024]{2,1,0:T(8,128)S(1)} %copy-done.15, f32[2,256,1024]{2,1,0:T(8,128)S(1)} %divide_add_fusion.1, f32[1,256,1024]{2,1,0:T(8,128)S(1)} %get-tuple-element.19, f32[1,256,1024]{2,1,0:T(8,128)S(1)} %select_bitcast_fusion.1, ...), kind=kOutput, calls=%fused_computation.42 | convolution fusion | flops 6461849600 | bytes 14684672 | tf_op jit(solution)/shard_map/dot_general | solution.py:46
  493.1 4.1 copy.81
  497.2 54.3 %all_to_all.114 = f32[2,256,1024]{1,0,2:T(2,128)S(1)} all-to-all(f32[2,256,1024]{1,0,2:T(2,128)} %copy.81), channel_id=1, replica_groups=mesh['tm'=8,'rows'=4] {'tm'}, dimensions={2} | all-to-all | bytes 4194304 | tf_op jit(solution)/shard_map/all_to_all | solution.py:192
  553.0 2.9 copy.83
  555.9 8.7 %slice_bitcast_fusion.3 = (f32[1,16,256,32]{3,2,1,0:T(8,128)}, f32[1,16,256,32]{3,2,1,0:T(8,128)}, f32[1,16,256,32]{3,2,1,0:T(8,128)}, f32[1,16,256,32]{3,2,1,0:T(8,128)}) fusion(f32[16,256,128]{2,1,0:T(8,128)} %bitcast.238), kind=kLoop, calls=%fused_computation.90 | loop fusion | bytes 4194304 | tf_op jit(solution)/shard_map/stack | solution.py:190
  566.7 2.2 copy.85
  568.9 3.0 copy.86
  571.9 3.0 copy.87
  576.2 29.0 %all_to_all.115 = f32[4,16,256,32]{2,3,1,0:T(8,128)} all-to-all(f32[4,16,256,32]{2,3,1,0:T(8,128)S(1)} %pad_maximum_fusion.1), channel_id=1, replica_groups=mesh['tm'=8,'rows'=4] {'rows'}, dimensions={0} | all-to-all | bytes 4194304 | tf_op jit(solution)/shard_map/all_to_all | solution.py:189
  605.2 6.3 copy.88
  611.5 7.0 reshape_reshape.7
  618.4 6.0 dot_general.72
  624.5 6.4 copy.89
  630.9 5.0 fusion.107
  635.9 33.4 %fusion.58 = f32[2,16,1024,32]{2,3,1,0:T(8,128)S(1)} fusion(f32[2,16,1024,32]{2,1,3,0:T(8,128)S(1)} %fusion.107, s32[1024]{0:T(1024)S(1)} %copy-done.16), kind=kOutput, calls=%fused_computation.75 | convolution fusion | flops 12899581952 | bytes 8392704 | tf_op jit(solution)/shard_map/kn,afnc->afkc/dot_general | solution.py:56
  670.5 30.7 %fusion.63 = f32[2,16,1024,32]{2,3,1,0:T(8,128)} fusion(f32[1,16,1024,32]{2,3,1,0:T(8,128)S(1)} %get-tuple-element.11, f32[1,16,1024,32]{2,3,1,0:T(8,128)S(1)} %get-tuple-element.10, f32[1024]{0:T(1024)S(1)} %select_multiply_fusion, s32[1024]{0:T(1024)S(1)} %copy-done.16), kind=kOutput, calls=%fused_computation.76 | convolution fusion | flops 12901679104 | bytes 8396800 | tf_op jit(solution)/shard_map/kn,afnc->afkc/dot_general | solution.py:56
  701.2 10.5 %copy.92 = f32[2,16,1024,32]{3,2,1,0:T(8,128)} copy(f32[2,16,1024,32]{2,3,1,0:T(8,128)} %fusion.63) | data formatting | bytes 8388608 | tf_op jit(solution)/shard_map/kn,afnc->afkc/transpose | solution.py:56
  711.6 11.7 %reshape.507 = f32[32,32768]{1,0:T(8,128)} reshape(f32[2,16,1024,32]{3,2,1,0:T(8,128)} %copy.92) | data formatting | bytes 8388608 | tf_op jit(solution)/shard_map/reshape | solution.py:76
  723.4 9.9 %dot_general.77 = f32[1024,32,32]{1,0,2:T(8,128)} reshape(f32[32768,32]{0,1:T(8,128)} %bitcast.241) | data formatting | bytes 8388608 | tf_op jit(solution)/shard_map/dot_general | solution.py:75
  733.2 11.7 %copy.93 = f32[1024,32,32]{0,2,1:T(8,128)} copy(f32[1024,32,32]{1,0,2:T(8,128)} %dot_general.77) | data formatting | bytes 8388608 | tf_op jit(solution)/shard_map/dot_general | solution.py:75
  744.9 4.1 fusion.163
  750.3 51.4 %all_to_all.116 = f32[16,1024,32]{1,2,0:T(8,128)S(1)} all-to-all(f32[16,1024,32]{1,2,0:T(8,128)S(1)} %copy.94), channel_id=1, replica_groups=mesh['tm'=8,'rows'=4] {'tm'}, dimensions={0} | all-to-all | bytes 4194304 | tf_op jit(solution)/shard_map/all_to_all | solution.py:217
  803.2 4.1 copy.96
  807.3 29.5 %all_to_all.117 = f32[2,1024,256]{2,0,1:T(2,128)S(1)} all-to-all(f32[2,1024,256]{2,0,1:T(2,128)} %copy.96), channel_id=1, replica_groups=mesh['tm'=8,'rows'=4] {'rows'}, dimensions={1} | all-to-all | bytes 4194304 | tf_op jit(solution)/shard_map/all_to_all | solution.py:216
  839.1 8.6 %divide_add_fusion = f32[2,256,1024]{2,1,0:T(8,128)} fusion(f32[2,256,1024]{2,1,0:T(8,128)S(1)} %divide_add_fusion.1, f32[2]{0:T(128)S(1)} %multiply_exponential_fusion, f32[2,256,1024]{2,1,0:T(8,128)S(1)} %bitcast.276, f32[1024,1024]{1,0:T(8,128)S(1)} %copy-done.12, pred[1024]{0:T(1024)(128)(4,1)S(1)} %compare_and_fusion), kind=kOutput, calls=%fused_computation.131 | convolution fusion | flops 6444548096 | bytes 10486792 | tf_op jit(solution)/shard_map/dot_general | solution.py:46
  (149 shorter events, 73.9 us)
Async XLA Ops:
  0.0 16.0 %copy-start = (f32[8,128,128]{2,1,0:T(8,128)S(1)}, f32[8,128,128]{2,1,0:T(8,128)}, u32[]{:S(2)}) copy-start(f32[8,128,128]{2,1,0:T(8,128)} %param.8) | copy-start | bytes 1572868
  0.0 73.3 %collective-permute-start = (f32[256,1024]{1,0:T(8,128)}, f32[256,1024]{1,0:T(8,128)}, u32[]{:S(2)}, u32[]{:S(2)}) collective-permute-start(f32[256,1024]{1,0:T(8,128)} %param.6), channel_id=1, source_target_pairs={{0,4},{4,8},{8,12},{12,16},{16,20},{20,24},{24,28},{1,5},{5,9},{9,... | collective-permute-start | bytes 3145736 | tf_op jit(solution)/shard_map/ppermute | solution.py:31
  7.4 61.9 %collective-permute-start.1 = (f32[2,1,1024]{2,1,0:T(1,128)}, f32[2,1,1024]{2,1,0:T(1,128)S(1)}, u32[]{:S(2)}, u32[]{:S(2)}) collective-permute-start(f32[2,1,1024]{2,1,0:T(1,128)} %broadcast_in_dim.376), channel_id=1, source_target_pairs={{0,1},{1,2},{2,3},{4,5},{5,6},{6,7},{8,9},{9,10},{10,11},{12,13},{... | collective-permute-start | bytes 24584 | tf_op jit(solution)/shard_map/ppermute | solution.py:20
  9.4 59.9 %collective-permute-start.2 = (f32[2,1,1024]{2,1,0:T(1,128)}, f32[2,1,1024]{2,1,0:T(1,128)S(1)}, u32[]{:S(2)}, u32[]{:S(2)}) collective-permute-start(f32[2,1,1024]{2,1,0:T(1,128)} %broadcast_in_dim.377), channel_id=1, source_target_pairs={{1,0},{2,1},{3,2},{5,4},{6,5},{7,6},{9,8},{10,9},{11,10},{13,12},{... | collective-permute-start | bytes 24584 | tf_op jit(solution)/shard_map/ppermute | solution.py:23
  25.6 1.4 copy-start.2
  42.7 10.6 %copy-start.17 = (s32[258]{0:T(512)S(1)}, s32[258]{0:T(512)}, u32[]{:S(2)}) copy-start(s32[258]{0:T(512)} %fusion.170) | copy-start | bytes 3100
  42.7 10.6 %copy-start.20 = (f32[4]{0:T(128)S(1)}, f32[4]{0:T(128)}, u32[]{:S(2)}) copy-start(f32[4]{0:T(128)} %param.10) | copy-start | bytes 52
  42.7 11.3 %copy-start.19 = (f32[4]{0:T(128)S(1)}, f32[4]{0:T(128)}, u32[]{:S(2)}) copy-start(f32[4]{0:T(128)} %param.11) | copy-start | bytes 52
  42.7 12.0 %copy-start.18 = (s32[258]{0:T(512)S(1)}, s32[258]{0:T(512)}, u32[]{:S(2)}) copy-start(s32[258]{0:T(512)} %iota_add_fusion) | copy-start | bytes 3100
  42.7 12.0 %copy-start.3 = (s32[8,8]{1,0:T(8,128)S(1)}, s32[8,8]{1,0:T(8,128)}, u32[]{:S(2)}) copy-start(s32[8,8]{1,0:T(8,128)} %param.9) | copy-start | bytes 772
  45.0 10.8 %copy-start.21 = (pred[258]{0:T(512)(128)(4,1)S(1)}, pred[258]{0:T(512)(128)(4,1)}, u32[]{:S(2)}) copy-start(pred[258]{0:T(512)(128)(4,1)} %compare_and_fusion.1) | copy-start | bytes 778
  67.6 2.0 copy-start.6
  68.0 1.4 copy-start.4
  69.3 1.2 copy-start.8
  70.5 1.2 copy-start.13
  73.2 1.6 copy-start.14
  73.2 1.6 copy-start.16
  166.8 5.3 copy-start.10
  176.3 30.2 %all-to-all-start.1 = ((f32[4,16,256,32]{2,3,1,0:T(8,128)}), f32[4,16,256,32]{2,3,1,0:T(8,128)S(1)}, u32[]{:S(2)}, u32[]{:S(2)}) async-start(f32[4,16,256,32]{2,3,1,0:T(8,128)} %pad_maximum_fusion), calls=%async_computation.1 | async-start | bytes 4194304 | tf_op jit(solution)/shard_map/all_to_all | solution.py:189
  399.0 29.4 %all-to-all-start.3 = ((f32[2,1024,256]{2,0,1:T(2,128)}), f32[2,1024,256]{2,0,1:T(2,128)S(1)}, u32[]{:S(2)}, u32[]{:S(2)}) async-start(f32[2,1024,256]{2,0,1:T(2,128)} %copy.77), calls=%async_computation.3 | async-start | bytes 4194304 | tf_op jit(solution)/shard_map/all_to_all | solution.py:216
  428.5 2.2 copy-start.11
  428.6 2.4 copy-start.5
  438.3 7.1 copy-start.7
  438.3 7.1 copy-start.9
  438.4 7.0 collective-permute-start.4
  440.1 5.2 collective-permute-start.5
  441.6 25.5 %collective-permute-start.3 = (f32[256,1024]{1,0:T(8,128)S(1)}, f32[256,1024]{1,0:T(8,128)S(1)}, u32[]{:S(2)}, u32[]{:S(2)}) collective-permute-start(f32[256,1024]{1,0:T(8,128)S(1)} %get-tuple-element.18), channel_id=1, source_target_pairs={{0,4},{4,8},{8,12},{12,16},{16,20},{20,24},{24,28},{1,5},{5,9},{9,... | collective-permute-start | bytes 3145736 | tf_op jit(solution)/shard_map/ppermute | solution.py:31
  447.8 19.5 %copy-start.15 = (f32[2,256,1024]{2,1,0:T(8,128)S(1)}, f32[2,256,1024]{2,1,0:T(8,128)}, u32[]{:S(2)}) copy-start(f32[2,256,1024]{2,1,0:T(8,128)} %select_add_fusion) | copy-start | bytes 6291460
  836.9 2.2 copy-start.12
  839.1 8.6 %copy-start.1 = (f32[8,128,128]{2,1,0:T(8,128)S(1)}, f32[8,128,128]{2,1,0:T(8,128)}, u32[]{:S(2)}) copy-start(f32[8,128,128]{2,1,0:T(8,128)} %param.8) | copy-start | bytes 1572868
